TPU v7x, 256 devices: a whole 4x4x8 slice. The times are simulated.
256 devices in a mesh: seq: 64 (over z, x_lo, y), heads: 4 (over x_hi, core).
Axes of the slice: x: 4 (x_hi: 2, x_lo: 2; x = x_hi * 2 + x_lo), y: 4, z: 8, core: 2. Of those that a mesh axis runs over, the one named last changes fastest.
Arguments:
- queries: bfloat16 [8192, 24576], P('seq', 'heads'), may hold values from -8 to 8
- latent: bfloat16 [8192, 576], P(('seq', 'heads')), may hold values from -8 to 8
- w_uk: bfloat16 [128, 128, 512], P('heads'), may hold values from -0.5 to 0.5
- w_uv: bfloat16 [128, 512, 128], P('heads'), may hold values from -0.75 to 0.75
- doc_lengths: int32 [32], replicated, may hold values from 1 to 1024, as said below
Outputs:
- attention_out: bfloat16 [8192, 16384], P('seq', 'heads')
Inputs may be any that keep to these rules, and one draw needn't show every extreme that they name: `doc_lengths`: the 32 lengths sum to 8192; the next to last document has exactly 1024 tokens and the last one at most 32.
All inputs are finite; a program needn't handle non-finite values.
Results may differ from a plain program's by a relative error of at most 0.0085.
Values may be sent and summed in bfloat16 or wider, within the bound.
A program may use at most 320 MiB of HBM per device.

v0:
```python
import jax
import jax.numpy as jnp
from jax import lax
from jax.sharding import PartitionSpec as P

SPAN = 8


far_negative = -1e30


def from_behind(x, axis, by):
    length = lax.axis_size(axis)
    pairs = [(i, i + by) for i in range(length) if 0 <= i + by < length]
    return lax.ppermute(x, axis, pairs)


def document_of(doc_ends, positions):
    return jnp.sum((doc_ends[None, :] <= positions[:, None]).astype(jnp.int32), axis=1)


def reach_back(own_block):
    held = own_block[None]
    stride = 1
    while stride < SPAN:
        held = jnp.concatenate([from_behind(held, "seq", stride), held], axis=0)
        stride = stride * 2
    farthest = from_behind(own_block, "seq", SPAN)
    return jnp.concatenate([farthest[None], held], axis=0)


def per_device(queries, latent, w_uk, w_uv, doc_lengths):
    heads_dev, nope_width, latent_rank = w_uk.shape
    value_width = w_uv.shape[2]
    tok_rows = queries.shape[0]
    query_width = queries.shape[1] // heads_dev
    score_scale = query_width ** (-0.5)
    query_heads = queries.reshape(tok_rows, heads_dev, query_width)
    absorbed = jnp.einsum(
        "thd,hdl->thl", query_heads[:, :, :nope_width], w_uk, preferred_element_type=jnp.float32
    ).astype(jnp.bfloat16)
    joined = jnp.concatenate([absorbed, query_heads[:, :, nope_width:]], axis=2)
    own_rows = lax.all_gather(latent, "heads", axis=0, tiled=True)
    window = reach_back(own_rows)
    first_pos = lax.axis_index("seq") * tok_rows
    doc_ends = jnp.cumsum(doc_lengths)
    query_pos = first_pos + jnp.arange(tok_rows, dtype=jnp.int32)
    key_pos = first_pos - SPAN * tok_rows + jnp.arange((SPAN + 1) * tok_rows, dtype=jnp.int32)
    query_doc = document_of(doc_ends, query_pos)
    key_doc = document_of(doc_ends, key_pos)
    allowed = (
        (key_doc[None, :] == query_doc[:, None])
        & (key_pos[None, :] <= query_pos[:, None])
        & (key_pos[None, :] >= 0)
    )
    allowed = allowed.reshape(tok_rows, SPAN + 1, tok_rows)
    value_rows = window[:, :, :latent_rank]
    raw_scores = jnp.einsum("thl,jkl->thjk", joined, window, preferred_element_type=jnp.float32)
    scores = jnp.where(allowed[:, None], raw_scores * score_scale, far_negative)
    row_top = jnp.max(scores, axis=(2, 3), keepdims=True)
    exponent = jnp.exp(scores - row_top)
    row_total = jnp.sum(exponent, axis=(2, 3))
    weights = exponent.astype(jnp.bfloat16)
    mixed_sum = jnp.einsum("thjk,jkl->thl", weights, value_rows, preferred_element_type=jnp.float32)
    attended = (mixed_sum / row_total[:, :, None]).astype(jnp.bfloat16)
    projected = jnp.einsum("thl,hlv->thv", attended, w_uv, preferred_element_type=jnp.float32)
    return projected.astype(jnp.bfloat16).reshape(tok_rows, heads_dev * value_width)


def solution(mesh):
    return jax.shard_map(
        per_device,
        mesh=mesh,
        in_specs=(
            P("seq", "heads"),
            P(("seq", "heads"), None),
            P("heads", None, None),
            P("heads", None, None),
            P(),
        ),
        out_specs=P("seq", "heads"),
        check_vma=False,
    )
```

profile of v0, /device:TPU:128, one launch (start us, length us, event | category | flops | bytes accessed | tf_op | source)
XLA Modules:
  0.0 93.0 jit_solution(16066146308441265323)
XLA Ops:
  0.0 7.2 %all_gather.3 = bf16[128,576]{1,0:T(8,128)(2,1)S(1)} all-gather(bf16[32,576]{1,0:T(8,128)(2,1)} %param.6), channel_id=1, replica_groups=mesh['seq'=64,'heads'=4] {'heads'}, dimensions={0}, use_global_device_ids=true | all-gather | bytes 184320 | tf_op jit(solution)/shard_map/all_gather | solution.py:43
  7.2 0.1 copy.39
  7.4 2.9 %collective-permute-start = (bf16[128,576]{0,1:T(8,128)(2,1)S(1)}, bf16[128,576]{0,1:T(8,128)(2,1)S(1)}, u32[]{:S(2)}, u32[]{:S(2)}) collective-permute-start(bf16[128,576]{0,1:T(8,128)(2,1)S(1)} %copy.39), channel_id=1, source_target_pairs={{0,32},{4,36},{8,40},{12,44},{16,48},{20,52},{24,56},{28,60},{32,6... | collective-permute-start | bytes 442376 | tf_op jit(solution)/shard_map/ppermute | solution.py:15
  10.3 3.5 %collective-permute-start.1 = (bf16[1,128,576]{1,2,0:T(8,128)(2,1)S(1)}, bf16[1,128,576]{1,2,0:T(8,128)(2,1)S(1)}, u32[]{:S(2)}, u32[]{:S(2)}) collective-permute-start(bf16[1,128,576]{1,2,0:T(8,128)(2,1)S(1)} %bitcast.40), channel_id=1, source_target_pairs={{0,4},{4,8},{8,12},{12,16},{16,20},{20,24},{24,28},{28,32},{32,36}... | collective-permute-start | bytes 442376 | tf_op jit(solution)/shard_map/ppermute | solution.py:15
  13.8 0.7 copy.35
  14.6 0.1 reduce-window.8
  14.6 0.1 reduce
  14.7 1.9 %copy.36 = bf16[128,6144]{0,1:T(8,128)(2,1)S(1)} copy(bf16[128,6144]{1,0:T(8,128)(2,1)} %param.5) | data formatting | bytes 3145728 | tf_op args[0]
  16.6 0.1 convert_reduce_fusion.1
  16.7 6.4 %collective-permute-done.1 = bf16[1,128,576]{1,2,0:T(8,128)(2,1)S(1)} collective-permute-done((bf16[1,128,576]{1,2,0:T(8,128)(2,1)S(1)}, bf16[1,128,576]{1,2,0:T(8,128)(2,1)S(1)}, u32[]{:S(2)}, u32[]{:S(2)}) %collective-permute-start.1) | collective-permute-done | bytes 147488 | tf_op jit(solution)/shard_map/ppermute | solution.py:15
  23.1 1.9 %collective-permute-start.2 = (bf16[2,128,576]{1,2,0:T(8,128)(2,1)S(1)}, bf16[2,128,576]{1,2,0:T(8,128)(2,1)S(1)}, u32[]{:S(2)}, u32[]{:S(2)}) collective-permute-start(bf16[2,128,576]{1,2,0:T(8,128)(2,1)S(1)} %pad_maximum_fusion.1), channel_id=1, source_target_pairs={{0,8},{4,12},{8,16},{12,20},{16,24},{20,28},{24,32},{28,36},{32,40... | collective-permute-start | bytes 884744 | tf_op jit(solution)/shard_map/ppermute | solution.py:15
  25.1 3.5 %convert_bitcast_fusion = bf16[128,32,512]{0,2,1:T(8,128)(2,1)S(1)} fusion(bf16[32,128,512]{2,1,0:T(8,128)(2,1)} %param.7, bf16[128,32,192]{0,2,1:T(8,128)(2,1)S(1)} %bitcast.38), kind=kOutput, calls=%fused_computation.16 | convolution fusion | flops 538968064 | bytes 9437184 | tf_op jit(solution)/shard_map/thd,hdl->thl/dot_general | solution.py:39
  28.6 9.3 %collective-permute-done.2 = bf16[2,128,576]{1,2,0:T(8,128)(2,1)S(1)} collective-permute-done((bf16[2,128,576]{1,2,0:T(8,128)(2,1)S(1)}, bf16[2,128,576]{1,2,0:T(8,128)(2,1)S(1)}, u32[]{:S(2)}, u32[]{:S(2)}) %collective-permute-start.2) | collective-permute-done | bytes 294944 | tf_op jit(solution)/shard_map/ppermute | solution.py:15
  37.9 0.1 pad_maximum_fusion
  38.0 1.9 %collective-permute-start.3 = (bf16[4,128,576]{1,2,0:T(8,128)(2,1)S(1)}, bf16[4,128,576]{1,2,0:T(8,128)(2,1)S(1)}, u32[]{:S(2)}, u32[]{:S(2)}) collective-permute-start(bf16[4,128,576]{1,2,0:T(8,128)(2,1)S(1)} %pad_maximum_fusion), channel_id=1, source_target_pairs={{0,16},{4,20},{8,24},{12,28},{16,32},{20,36},{24,40},{28,44},{32,4... | collective-permute-start | bytes 1769480 | tf_op jit(solution)/shard_map/ppermute | solution.py:15
  40.0 0.1 convert_reduce_fusion
  40.1 0.7 and_and_fusion
  40.8 0.0 collective-permute-done
  40.8 15.0 %collective-permute-done.3 = bf16[4,128,576]{1,2,0:T(8,128)(2,1)S(1)} collective-permute-done((bf16[4,128,576]{1,2,0:T(8,128)(2,1)S(1)}, bf16[4,128,576]{1,2,0:T(8,128)(2,1)S(1)}, u32[]{:S(2)}, u32[]{:S(2)}) %collective-permute-start.3) | collective-permute-done | bytes 589856 | tf_op jit(solution)/shard_map/ppermute | solution.py:15
  55.9 0.1 constant_dynamic-update-slice_fusion.3
  56.1 12.2 %fusion = (f32[128,32]{0,1:T(8,128)S(1)}, f32[128,32,9,128]{0,3,2,1:T(8,128)}) fusion(pred[128,9,128]{0,2,1:T(8,128)(4,1)S(1)} %and_and_fusion, bf16[9,128,576]{1,2,0:T(8,128)(2,1)S(1)} %constant_dynamic-update-slice_fusion, bf16[128,32,64]{0,2,1:T(8,128)(2,1)S(1)} %slice.13, bf16[128,32,512]{0,2,1:T(8,128)(2,1)S(1)} %convert_bitcast_fusion), kind=kOutput, calls=%fused_computation.2 | convolution fusion | flops 5459406848 | bytes 25083904 | tf_op jit(solution)/shard_map/thl,jkl->thjk/dot_general | solution.py:58
  68.2 10.3 %fusion.1 = f32[128,32]{0,1:T(8,128)S(1)} fusion(f32[128,32,9,128]{0,3,2,1:T(8,128)} %get-tuple-element.6, f32[128,32]{0,1:T(8,128)S(1)} %get-tuple-element.5, pred[128,9,128]{0,2,1:T(8,128)(4,1)S(1)} %and_and_fusion), kind=kLoop, calls=%fused_computation.3 | loop fusion | flops 18870272 | bytes 19054592 | tf_op jit(solution)/shard_map/reduce_sum | solution.py:62
  78.5 13.2 %fusion.19 = bf16[32,128,128]{1,2,0:T(8,128)(2,1)S(1)} fusion(bf16[32,512,128]{2,1,0:T(8,128)(2,1)} %param.8, f32[128,32]{0,1:T(8,128)S(1)} %fusion.1, f32[128,32,9,128]{0,3,2,1:T(8,128)} %get-tuple-element.6, f32[128,32]{0,1:T(8,128)S(1)} %get-tuple-element.5, pred[128,9,128]{0,2,1:T(8,128)(4,1)S(1)} %and_and_fusion, ...), kind=kOutput, calls=%fused_computation.18 | convolution fusion | flops 5392302080 | bytes 25477120 | tf_op jit(solution)/shard_map/thl,hlv->thv/dot_general | solution.py:66
  91.7 1.3 %copy.44 = bf16[128,4096]{1,0:T(8,128)(2,1)} copy(bf16[128,4096]{0,1:T(8,128)(2,1)S(1)} %bitcast.43) | data formatting | bytes 2097152 | tf_op jit(solution)/shard_map/reshape | solution.py:67
  (10 shorter events, 0.2 us)
Async XLA Ops:
  7.4 33.5 %collective-permute-start = (bf16[128,576]{0,1:T(8,128)(2,1)S(1)}, bf16[128,576]{0,1:T(8,128)(2,1)S(1)}, u32[]{:S(2)}, u32[]{:S(2)}) collective-permute-start(bf16[128,576]{0,1:T(8,128)(2,1)S(1)} %copy.39), channel_id=1, source_target_pairs={{0,32},{4,36},{8,40},{12,44},{16,48},{20,52},{24,56},{28,60},{32,6... | collective-permute-start | bytes 442376 | tf_op jit(solution)/shard_map/ppermute | solution.py:15
  10.3 12.8 %collective-permute-start.1 = (bf16[1,128,576]{1,2,0:T(8,128)(2,1)S(1)}, bf16[1,128,576]{1,2,0:T(8,128)(2,1)S(1)}, u32[]{:S(2)}, u32[]{:S(2)}) collective-permute-start(bf16[1,128,576]{1,2,0:T(8,128)(2,1)S(1)} %bitcast.40), channel_id=1, source_target_pairs={{0,4},{4,8},{8,12},{12,16},{16,20},{20,24},{24,28},{28,32},{32,36}... | collective-permute-start | bytes 442376 | tf_op jit(solution)/shard_map/ppermute | solution.py:15
  23.1 14.8 %collective-permute-start.2 = (bf16[2,128,576]{1,2,0:T(8,128)(2,1)S(1)}, bf16[2,128,576]{1,2,0:T(8,128)(2,1)S(1)}, u32[]{:S(2)}, u32[]{:S(2)}) collective-permute-start(bf16[2,128,576]{1,2,0:T(8,128)(2,1)S(1)} %pad_maximum_fusion.1), channel_id=1, source_target_pairs={{0,8},{4,12},{8,16},{12,20},{16,24},{20,28},{24,32},{28,36},{32,40... | collective-permute-start | bytes 884744 | tf_op jit(solution)/shard_map/ppermute | solution.py:15
  38.0 17.9 %collective-permute-start.3 = (bf16[4,128,576]{1,2,0:T(8,128)(2,1)S(1)}, bf16[4,128,576]{1,2,0:T(8,128)(2,1)S(1)}, u32[]{:S(2)}, u32[]{:S(2)}) collective-permute-start(bf16[4,128,576]{1,2,0:T(8,128)(2,1)S(1)} %pad_maximum_fusion), channel_id=1, source_target_pairs={{0,16},{4,20},{8,24},{12,28},{16,32},{20,36},{24,40},{28,44},{32,4... | collective-permute-start | bytes 1769480 | tf_op jit(solution)/shard_map/ppermute | solution.py:15
where the time goes:
time: 93.3 us; the launch traced here: 93 us
  waiting for transfers between devices  30.7 us (33%)
  matrix products  28.9 us (31%)
  other arithmetic  11.5 us (12%)
  starting transfers between devices  10.3 us (11%)
  blocking collectives  7.21 us (8%)
  local copies, waits for them, and re-layouts  4.31 us (5%)
    ppermute x4, waiting for transfers between devices, from_behind(): return lax.ppermute(x, axis, pairs)  30.7 us
    dot_general x1, matrix products, per_device(): jnp.einsum('thl,hlv->thv', attended, w_uv, preferred_element_type=jnp.flo...  13.2 us
    dot_general x1, matrix products, per_device(): jnp.einsum('thl,jkl->thjk', joined, window, preferred_element_type=jnp.fl...  12.2 us
    reduce_sum x1, other arithmetic, per_device(): row_total = jnp.sum(exponent, axis=(2, 3))  10.3 us
    ppermute x4, starting transfers between devices, from_behind(): return lax.ppermute(x, axis, pairs)  10.3 us
    all_gather x1, blocking collectives, per_device(): own_rows = lax.all_gather(latent, 'heads', axis=0, tiled=True)  7.21 us
    dot_general x1, matrix products, per_device(): jnp.einsum('thd,hdl->thl', query_heads[:, :, :nope_width], w_uk, preferre...  3.52 us
    unnamed x5, local copies, waits for them, and re-layouts  2.06 us
  transfers between devices with their start and end apart: 4, of which 3 were waited for; matrix products, arithmetic and copies ran while one was open for 8% of the time, Pallas kernels for 0%

commit v1 on v0

v1 whole, which is shorter than its diff:
```python
import functools
import math

import jax
import jax.numpy as jnp
from jax import lax
from jax.experimental import pallas as pl
from jax.experimental.pallas import tpu as pltpu
from jax.sharding import PartitionSpec as P

SPAN = 8
SLOTS = SPAN + 1
FAR = -1e30
MESH = pl.DeviceIdType.MESH
CHUNKS = ((0,), (1, 2), (3, 4), (5, 6), (7, 8))


def kernel(dims, doc_ref, q_hbm, lat_hbm, wuk_hbm, wuv_hbm, out_hbm,
           q_v, wuk_v, wuv_v, kv, kk, joined, m_ref, l_ref, acc_ref, out_v,
           q_sem, wuk_sem, wuv_sem, lat_sem, out_sem,
           send_d, recv_d, send_p, recv_p):
    n_seq, heads, nope, rope, rank, vdim, toks, piece, groups, docs = dims
    width = nope + rope
    scale = (width ** -0.5) * math.log2(math.e)
    per = heads // groups
    rows = per * toks

    s = lax.axis_index("seq")
    hd = lax.axis_index("heads")
    core = hd % 2
    xh = hd // 2
    mate = xh * 2 + (1 - core)

    def own_rows(h):
        return pl.ds(pl.multiple_of(h * piece, piece), piece)

    lat_copy = pltpu.make_async_copy(lat_hbm, kv.at[0, own_rows(hd)], lat_sem)
    lat_copy.start()
    q_copies, wuk_copies, wuv_copies = [], [], []
    for g in range(groups):
        cols = pl.ds(g * per * width, per * width)
        q_copies.append(pltpu.make_async_copy(q_hbm.at[:, cols], q_v.at[:, cols], q_sem.at[g]))
        hs = pl.ds(g * per, per)
        wuk_copies.append(pltpu.make_async_copy(wuk_hbm.at[hs], wuk_v.at[hs], wuk_sem.at[g]))
        wuv_copies.append(pltpu.make_async_copy(wuv_hbm.at[hs], wuv_v.at[hs], wuv_sem.at[g]))
        q_copies[-1].start()
        wuk_copies[-1].start()

    barrier = pltpu.get_barrier_semaphore()
    pl.semaphore_signal(barrier, inc=1, device_id=(s, mate), device_id_type=MESH)
    for d in range(SLOTS):
        src = (s + n_seq - d) % n_seq
        for flip in ((1,) if d == 0 else (0, 1)):
            other = (xh + flip) % 2 * 2 + core
            pl.semaphore_signal(barrier, inc=1, device_id=(src, other), device_id_type=MESH)

    lane = lax.broadcasted_iota(jnp.int32, (1, toks), 1)
    tok_pos = s * toks + lane
    start = jnp.zeros((1, toks), jnp.int32)
    end = jnp.int32(0)
    for d in range(docs):
        end = end + doc_ref[d]
        start = jnp.where(end <= tok_pos, end, start)

    eye = (lax.broadcasted_iota(jnp.int32, (toks, toks), 0)
           == lax.broadcasted_iota(jnp.int32, (toks, toks), 1)).astype(jnp.float32).astype(jnp.bfloat16)

    lat_copy.wait()
    pl.semaphore_wait(barrier, 2 * SLOTS)

    sends = []

    def remote(src, dst, ss, rs, dev):
        return pltpu.make_async_remote_copy(
            src_ref=src, dst_ref=dst, send_sem=ss, recv_sem=rs, device_id=dev, device_id_type=MESH)

    def to_mate(d, h, k):
        ref = kv.at[d, own_rows(h)]
        return remote(ref, ref, send_p.at[d, k], recv_p.at[d, k], (s, mate))

    own = kv.at[0, own_rows(hd)]
    copy = to_mate(0, hd, 0)
    copy.start()
    sends.append(copy)
    direct = {}
    for d in range(SLOTS):
        dst_seq = (s + d) % n_seq
        for flip in ((1,) if d == 0 else (0, 1)):
            other = (xh + flip) % 2 * 2 + core
            copy = remote(own, kv.at[d, own_rows(hd)], send_d.at[d, flip], recv_d.at[d, flip], (dst_seq, other))
            copy.start()
            sends.append(copy)
    for g in range(groups):
        wuv_copies[g].start()

    def arrived(d, flip):
        other = (xh + flip) % 2 * 2 + core
        ref = kv.at[d, own_rows(other)]
        return remote(ref, ref, send_d.at[d, flip], recv_d.at[d, flip], (s, mate)), other

    def forward(d):
        for flip in ((1,) if d == 0 else (0, 1)):
            copy, other = arrived(d, flip)
            copy.wait_recv()
            relay = to_mate(d, other, flip)
            relay.start()
            sends.append(relay)

    def from_mate(d):
        for flip in (0, 1):
            other = (xh + flip) % 2 * 2 + (1 - core)
            to_mate(d, other, flip).wait_recv()

    low = lax.broadcasted_iota(jnp.int32, (toks, 128), 1) < rope
    for g in range(groups):
        q_copies[g].wait()
        wuk_copies[g].wait()

        def pair(i, carry):
            p = g * (per // 2) + i
            q3 = q_v[:, pl.ds(pl.multiple_of(p * 2 * width, 128), 2 * width)]
            q_even = q3[:, :nope]
            q_odd = q3[:, width:width + nope]
            zero = jnp.zeros((toks, 128), jnp.bfloat16)
            ropes = (jnp.where(low, q3[:, 128:256], zero), jnp.where(low, zero, q3[:, 256:384]))
            for j, qn in enumerate((q_even, q_odd)):
                h = 2 * p + j
                at = pl.ds(pl.multiple_of(h * toks, toks), toks)
                a = jnp.dot(qn, wuk_v[h], preferred_element_type=jnp.float32)
                joined[at, :rank] = a.astype(jnp.bfloat16)
                joined[at, rank:rank + 128] = ropes[j]
                joined[at, rank + 128:rank + 256] = eye
            return carry

        lax.fori_loop(0, per // 2, pair, 0)

    forward(0)

    def keys_of(c):
        buf = kk.at[c % 2]
        for j, d in enumerate(CHUNKS[c]):
            block = kv[d]
            at = pl.ds(j * toks, toks)
            key_pos = (s - d) * toks + lax.broadcasted_iota(jnp.int32, (toks, toks), 0)
            ok = (key_pos >= start) & (key_pos <= tok_pos)
            bias = jnp.where(ok, jnp.float32(0), jnp.float32(FAR)).astype(jnp.bfloat16)
            rope_rows = block[:, rank:rank + rope]
            buf[at, :rank] = block[:, :rank]
            buf[at, rank:rank + 128] = jnp.concatenate([rope_rows, rope_rows], axis=1)
            buf[at, rank + 128:rank + 256] = bias

    def score(c, i):
        n = len(CHUNKS[c]) * toks
        return lax.dot_general(joined[pl.ds(i * rows, rows), :], kk[c % 2, :n, :],
                               (((1,), (1,)), ((), ())), preferred_element_type=jnp.float32)

    def mix(c, i, sc):
        n = len(CHUNKS[c]) * toks
        at = pl.ds(i * rows, rows)
        top = jnp.max(sc, axis=1, keepdims=True)
        values = kk[c % 2, :n, :rank]
        if c == 0:
            m_new = jnp.broadcast_to(top, (rows, 128))
        else:
            m_old = m_ref[at, :]
            m_new = jnp.maximum(m_old, top)
        ps = [jnp.exp2((sc[:, k * 128:(k + 1) * 128] - m_new) * scale) for k in range(n // 128)]
        total = functools.reduce(lambda a, b: a + b, ps)
        p = ps[0] if len(ps) == 1 else jnp.concatenate(ps, axis=1)
        mixed = jnp.dot(p.astype(jnp.bfloat16), values, preferred_element_type=jnp.float32)
        if c > 0:
            alpha = jnp.exp2((m_old - m_new) * scale)
            total = total + l_ref[at, :] * alpha
            mixed = mixed + acc_ref[at, :] * jnp.concatenate([alpha] * (rank // 128), axis=1)
        if c < len(CHUNKS) - 1:
            m_ref[at, :] = m_new
            l_ref[at, :] = total
            acc_ref[at, :] = mixed
            return
        whole = jnp.sum(total, axis=1, keepdims=True)
        attended = (mixed * (1.0 / whole)).astype(jnp.bfloat16)
        for j in range(per):
            h = i * per + j
            out_v[:, h * vdim:(h + 1) * vdim] = jnp.dot(
                attended[j * toks:(j + 1) * toks, :], wuv_v[h], preferred_element_type=jnp.float32
            ).astype(jnp.bfloat16)

    out_copies = []
    for c in range(len(CHUNKS)):
        for d in CHUNKS[c]:
            from_mate(d)
        keys_of(c)
        last = c == len(CHUNKS) - 1
        if last:
            for g in range(groups):
                wuv_copies[g].wait()
        sc = score(c, 0)
        for i in range(groups):
            ahead = score(c, i + 1) if i + 1 < groups else None
            mix(c, i, sc)
            sc = ahead
            if last:
                cols = pl.ds(i * per * vdim, per * vdim)
                copy = pltpu.make_async_copy(out_v.at[:, cols], out_hbm.at[:, cols], out_sem.at[i])
                copy.start()
                out_copies.append(copy)
            if i == groups // 2 - 1 and not last:
                for d in CHUNKS[c + 1]:
                    forward(d)
    for copy in sends:
        copy.wait_send()
    for copy in out_copies:
        copy.wait()


def per_device(n_seq, queries, latent, w_uk, w_uv, doc_lengths):
    heads, nope, rank = w_uk.shape
    vdim = w_uv.shape[2]
    toks = queries.shape[0]
    width = queries.shape[1] // heads
    rope = width - nope
    piece = latent.shape[0]
    groups = 4
    dims = (n_seq, heads, nope, rope, rank, vdim, toks, piece, groups, doc_lengths.shape[0])
    anywhere = pl.BlockSpec(memory_space=pl.ANY)
    dma = pltpu.SemaphoreType.DMA
    all_rows = heads * toks
    return pl.pallas_call(
        functools.partial(kernel, dims),
        out_shape=jax.ShapeDtypeStruct((toks, heads * vdim), jnp.bfloat16),
        in_specs=[pl.BlockSpec(memory_space=pltpu.SMEM)] + [anywhere] * 4,
        out_specs=anywhere,
        scratch_shapes=[
            pltpu.VMEM(queries.shape, jnp.bfloat16),
            pltpu.VMEM(w_uk.shape, jnp.bfloat16),
            pltpu.VMEM(w_uv.shape, jnp.bfloat16),
            pltpu.VMEM((SLOTS, toks, rank + rope), jnp.bfloat16),
            pltpu.VMEM((2, 2 * toks, rank + 256), jnp.bfloat16),
            pltpu.VMEM((all_rows, rank + 256), jnp.bfloat16),
            pltpu.VMEM((all_rows, 128), jnp.float32),
            pltpu.VMEM((all_rows, 128), jnp.float32),
            pltpu.VMEM((all_rows, rank), jnp.float32),
            pltpu.VMEM((toks, heads * vdim), jnp.bfloat16),
            dma((groups,)), dma((groups,)), dma((groups,)), dma, dma((groups,)),
            dma((SLOTS, 2)), dma((SLOTS, 2)), dma((SLOTS, 2)), dma((SLOTS, 2)),
        ],
        compiler_params=pltpu.CompilerParams(
            collective_id=0, has_side_effects=True, vmem_limit_bytes=60 * 1024 * 1024),
    )(doc_lengths, queries, latent, w_uk, w_uv)


def solution(mesh):
    return jax.shard_map(
        functools.partial(per_device, mesh.shape["seq"]),
        mesh=mesh,
        in_specs=(
            P("seq", "heads"),
            P(("seq", "heads"), None),
            P("heads", None, None),
            P("heads", None, None),
            P(),
        ),
        out_specs=P("seq", "heads"),
        check_vma=False,
    )
```

time: 93.3 us -> 42.3 us (0.45)
  the two profiles are of different devices: /device:TPU:128 before, /device:TPU:1 now
where the time goes in v1:
time: 42.3 us; the launch traced here: 42.2 us
  Pallas kernels  39.9 us (94%)
  local copies, waits for them, and re-layouts  2.29 us (5%)
    pallas_call x1, Pallas kernels, per_device(): pl.pallas_call(functools.partial(kernel, dims), out_shape=jax.ShapeDtypeS...  39.9 us
    unnamed x1, local copies, waits for them, and re-layouts  2.29 us

profile of v1, /device:TPU:1, one launch (start us, length us, event | category | flops | bytes accessed | tf_op | source)
XLA Modules:
  0.0 42.2 jit_solution(12208890196212524087)
XLA Ops:
  0.0 39.9 %shard_map.55 = bf16[128,4096]{1,0:T(8,128)(2,1)} custom-call(s32[32]{0:T(128)} %doc_ref.1, bf16[128,6144]{1,0:T(8,128)(2,1)} %q_hbm.1, bf16[32,576]{1,0:T(8,128)(2,1)} %lat_hbm.1, bf16[32,128,512]{2,1,0:T(8,128)(2,1)} %wuk_hbm.1, bf16[32,512,128]{2,1,0:T(8,128)(2,1)} %wuv_hbm.1), custom_call_target="tpu_custom_call" | custom-call | tf_op jit(solution)/shard_map/pallas_call | solution.py:228
  39.9 2.3 %copy.7 = bf16[128,4096]{1,0:T(8,128)(2,1)} copy(bf16[128,4096]{1,0:T(8,128)(2,1)} %shard_map.55) | data formatting | bytes 2097152

commit v2 on v0

v2 whole, which is shorter than its diff:
```python
import functools
import math

import jax
import jax.numpy as jnp
from jax import lax
from jax.experimental import pallas as pl
from jax.experimental.pallas import tpu as pltpu
from jax.sharding import PartitionSpec as P

SPAN = 8
SLOTS = SPAN + 1
PLANE = 8
NEAR = 3
FAR = -1e30
MESH = pl.DeviceIdType.MESH
SEGMENTS = (((0,),), ((1, 2), (3, 4)), ((5, 6), (7, 8)))
STRIP = 64
LANES = 256
TILE = 4


def kernel(dims, doc_ref, q_hbm, lat_hbm, wuk_hbm, wuv_hbm, out_v,
           q_v, wuk_v, wuv_v, kv, kk, joined, sc_ref, ring_a, ring_b, p_a, p_b, a_a, a_b, m_ref, l_ref, acc_ref, t_ref,
           q_sem, wuk_sem, wuv_sem, lat_sem,
           send_d, recv_d, send_p, recv_p, send_x):
    n_seq, heads, nope, rope, rank, vdim, toks, piece, groups, docs = dims
    width = nope + rope
    scale = (width ** -0.5) * math.log2(math.e)
    per = heads // groups
    rows = per * toks
    tile = TILE * toks
    tiles = heads // TILE
    ring, p_ref, a_ref = (ring_a, ring_b), (p_a, p_b), (a_a, a_b)

    s = lax.axis_index("seq")
    hd = lax.axis_index("heads")
    core = hd % 2
    xh = hd // 2
    mate = xh * 2 + (1 - core)
    spot = s % PLANE

    def holder(flip):
        return (xh + flip) % 2 * 2 + core

    def own_rows(h):
        return pl.ds(pl.multiple_of(h * piece, piece), piece)

    lat_copy = pltpu.make_async_copy(lat_hbm, kv.at[0, own_rows(hd)], lat_sem)
    lat_copy.start()
    q_copies, wuk_copies, wuv_copies = [], [], []
    for g in range(groups):
        cols = pl.ds(g * per * width, per * width)
        q_copies.append(pltpu.make_async_copy(q_hbm.at[:, cols], q_v.at[:, cols], q_sem.at[g]))
        hs = pl.ds(g * per, per)
        wuk_copies.append(pltpu.make_async_copy(wuk_hbm.at[hs], wuk_v.at[hs], wuk_sem.at[g]))
        wuv_copies.append(pltpu.make_async_copy(wuv_hbm.at[hs], wuv_v.at[hs], wuv_sem.at[g]))
        q_copies[-1].start()
        wuk_copies[-1].start()

    barrier = pltpu.get_barrier_semaphore()

    def greet(seq, h):
        pl.semaphore_signal(barrier, inc=1, device_id=(seq, h), device_id_type=MESH)

    def sends_direct(seq, d):
        inside = seq + d < n_seq
        if NEAR < d < SPAN:
            return jnp.logical_and(inside, seq % PLANE + d < PLANE)
        return inside

    def relays(seq, d):
        return jnp.logical_and(seq % PLANE + d >= SPAN, seq >= SPAN)

    greet(s, mate)
    greet(s, holder(1))
    greet(s, xh_other_mate := (1 - xh) * 2 + (1 - core))
    for d in range(1, SLOTS):
        direct_from = s - d
        ok = jnp.logical_and(s >= d, sends_direct(direct_from, d))

        @pl.when(ok)
        def _():
            greet(direct_from, holder(0))
            greet(direct_from, holder(1))

        if NEAR < d < SPAN:
            relay_from = s - d + SPAN
            ok_relay = jnp.logical_and(relay_from < n_seq, relays(relay_from, d))

            @pl.when(ok_relay)
            def _():
                greet(relay_from, holder(0))
                greet(relay_from, holder(1))

    expected = jnp.int32(3)
    for d in range(1, SLOTS):
        expected = expected + 2 * sends_direct(s, d).astype(jnp.int32)
        if NEAR < d < SPAN:
            expected = expected + 2 * relays(s, d).astype(jnp.int32)

    lane = lax.broadcasted_iota(jnp.int32, (1, toks), 1)
    tok_pos = s * toks + lane
    start = jnp.zeros((1, toks), jnp.int32)
    end = jnp.int32(0)
    for d in range(docs):
        end = end + doc_ref[d]
        start = jnp.where(end <= tok_pos, end, start)

    eye = (lax.broadcasted_iota(jnp.int32, (toks, toks), 0)
           == lax.broadcasted_iota(jnp.int32, (toks, toks), 1)).astype(jnp.float32).astype(jnp.bfloat16)
    low = lax.broadcasted_iota(jnp.int32, (toks, 128), 1) < rope
    for d in range(1, SLOTS):
        @pl.when(s < d)
        def _():
            kv[d] = jnp.zeros(kv.shape[1:], jnp.bfloat16)

    def absorb(g):
        q_copies[g].wait()
        wuk_copies[g].wait()
        zero = jnp.zeros((toks, 128), jnp.bfloat16)
        for p in range(g * per // 2, (g + 1) * per // 2):
            q3 = q_v[:, p * 2 * width:(p + 1) * 2 * width]
            ropes = (jnp.where(low, q3[:, 128:256], zero), jnp.where(low, zero, q3[:, 256:384]))
            ropes = [(x.astype(jnp.float32) * scale).astype(jnp.bfloat16) for x in ropes]
            for j, qn in enumerate((q3[:, :nope], q3[:, width:width + nope])):
                h = 2 * p + j
                at = pl.ds(h * toks, toks)
                a = jnp.dot(qn, wuk_v[h], preferred_element_type=jnp.float32)
                joined[at, :rank] = (a * scale).astype(jnp.bfloat16)
                joined[at, rank:rank + 128] = ropes[j]
                joined[at, rank + 128:rank + 256] = eye

    with jax.named_scope("absA"):
        for g in range(groups // 2):
            absorb(g)
    with jax.named_scope("bar"):
        lat_copy.wait()
        pl.semaphore_wait(barrier, expected)

    def remote(src, dst, ss, rs, dev):
        return pltpu.make_async_remote_copy(
            src_ref=src, dst_ref=dst, send_sem=ss, recv_sem=rs, device_id=dev, device_id_type=MESH)

    def to_mate(d, flip):
        ref = kv.at[d, own_rows(holder(flip))]
        return remote(ref, ref, send_p.at[d, flip], recv_p.at[d, flip], (s, mate))

    def outgoing(src, d, flip, seq):
        return remote(src, kv.at[d, own_rows(hd)], send_d.at[d, flip], recv_d.at[d, flip], (seq, holder(flip)))

    def arrived(d, flip):
        ref = kv.at[d, own_rows(holder(flip))]
        remote(ref, ref, send_d.at[d, flip], recv_d.at[d, flip], (s, mate)).wait_recv()

    own = kv.at[0, own_rows(hd)]
    first = [
        outgoing(own, 0, 1, s),
        remote(own, own, send_x, recv_p.at[0, 1], (s, xh_other_mate)),
        to_mate(0, 0),
    ]
    for copy in first:
        copy.start()
    def send(d, flips=(0, 1)):
        @pl.when(sends_direct(s, d))
        def _():
            for flip in flips:
                outgoing(own, d, flip, s + d).start()

    half = groups // 2
    with jax.named_scope("absB"):
        absorb(half)
    for d in range(1, NEAR + 1):
        send(d)
    send(SPAN, (0,))
    for g in range(groups):
        wuv_copies[g].start()
    with jax.named_scope("absC"):
        for g in range(half + 1, groups):
            absorb(g)
    for d in range(NEAR + 1, SPAN):
        send(d)
    send(SPAN, (1,))

    def pass_on():
        @pl.when(s >= SPAN)
        def _():
            with jax.named_scope("w8"):
                arrived(SPAN, 0)
            passed = kv.at[SPAN, own_rows(hd)]
            for d in range(NEAR + 1, SPAN):
                @pl.when(relays(s, d))
                def _():
                    for flip in (0, 1):
                        outgoing(passed, d, flip, s + d - SPAN).start()
            to_mate(SPAN, 0).start()

    def forward(d):
        with jax.named_scope(f"fw{d}"):
            @pl.when(s >= d)
            def _():
                for flip in ((1,) if d == SPAN else (0, 1)):
                    arrived(d, flip)
                    to_mate(d, flip).start()

    def from_mate(d):
        with jax.named_scope(f"mate{d}"):
            @pl.when(s >= d)
            def _():
                for flip in (0, 1):
                    ref = kv.at[d, own_rows((xh + flip) % 2 * 2 + (1 - core))]
                    remote(ref, ref, send_p.at[d, flip], recv_p.at[d, flip], (s, mate)).wait_recv()

    def keys_of(d):
        block = kv[d]
        at = pl.ds(d * toks, toks)
        key_pos = (s - d) * toks + lax.broadcasted_iota(jnp.int32, (toks, toks), 0)
        ok = (key_pos >= start) & (key_pos <= tok_pos)
        bias = jnp.where(ok, jnp.float32(0), jnp.float32(FAR)).astype(jnp.bfloat16)
        rope_rows = block[:, rank:rank + rope]
        kk[at, :rank] = block[:, :rank]
        kk[at, rank:rank + 128] = jnp.concatenate([rope_rows, rope_rows], axis=1)
        kk[at, rank + 128:rank + 256] = bias

    def score(chunk, at, store):
        n = len(chunk) * toks
        x = lax.dot_general(
            joined[at, :], kk[pl.ds(chunk[0] * toks, n), :],
            (((1,), (1,)), ((), ())), preferred_element_type=jnp.float32)
        store(x)
        top = functools.reduce(jnp.maximum, [x[:, k * 128:(k + 1) * 128] for k in range(n // 128)])
        m_ref[at, :] = top if chunk[0] == 0 else jnp.maximum(m_ref[at, :], top)

    def score_early(chunk, base, i):
        at = pl.ds(i * rows, rows)

        def store(x):
            sc_ref[at, pl.ds((chunk[0] - base) * toks, len(chunk) * toks)] = x
        score(chunk, at, store)

    def rows_of(i):
        return pl.ds(pl.multiple_of(i * tile, tile), tile)

    def score_last(chunk, i, odd):
        def store(x):
            ring[odd][:, :len(chunk) * toks] = x
        score(chunk, rows_of(i), store)

    def soften(early, late, i, odd, seg):
        last = seg == len(SEGMENTS) - 1
        for r in range(tile // STRIP):
            at = pl.ds(pl.multiple_of(i * tile + r * STRIP, STRIP), STRIP)
            here = slice(r * STRIP, (r + 1) * STRIP)
            top = jnp.broadcast_to(jnp.max(m_ref[at, :], axis=1, keepdims=True), (STRIP, 128))
            total = None
            for k in range(early + late):
                if k < early:
                    x = sc_ref[at, k * 128:(k + 1) * 128]
                else:
                    x = ring[odd][here, (k - early) * 128:(k - early + 1) * 128]
                p = jnp.exp2(x - top)
                total = p if total is None else total + p
                p_ref[odd][here, k * 128:(k + 1) * 128] = p.astype(jnp.bfloat16)
            if seg:
                alpha = jnp.exp2(t_ref[at, :] - top)
                total = total + l_ref[at, :] * alpha
            if last:
                inv = 1.0 / jnp.sum(total, axis=1, keepdims=True)
                a_ref[odd][here, :] = alpha * inv
                l_ref[at, :] = jnp.broadcast_to(inv, (STRIP, 128))
            else:
                l_ref[at, :] = total
                t_ref[at, :] = top
                if seg:
                    a_ref[odd][here, :] = alpha

    def mix(base, count, i, odd, seg):
        at = rows_of(i)
        attended = []
        for n in range(0, rank, LANES):
            cols = slice(n, n + LANES)
            mixed = jnp.dot(p_ref[odd][:, :count * toks], kk[pl.ds(base * toks, count * toks), cols],
                            preferred_element_type=jnp.float32)
            if seg == 0:
                acc_ref[at, cols] = mixed
                continue
            kept = acc_ref[at, cols] * jnp.concatenate([a_ref[odd][...]] * (LANES // 128), axis=1)
            if seg < len(SEGMENTS) - 1:
                acc_ref[at, cols] = kept + mixed
                continue
            inv = jnp.concatenate([l_ref[at, :]] * (LANES // 128), axis=1)
            attended.append((kept + mixed * inv).astype(jnp.bfloat16))
        if seg < len(SEGMENTS) - 1:
            return
        for j in range(TILE):
            h = i * TILE + j
            here = slice(j * toks, (j + 1) * toks)
            whole = jnp.concatenate([x[here] for x in attended], axis=1)
            out_v[:, pl.ds(pl.multiple_of(h * vdim, vdim), vdim)] = jnp.dot(
                whole, wuv_v[h], preferred_element_type=jnp.float32).astype(jnp.bfloat16)

    with jax.named_scope("w0"):
        arrived(0, 1)
        for flip in (0, 1):
            ref = kv.at[0, own_rows((xh + flip) % 2 * 2 + (1 - core))]
            remote(ref, ref, send_p.at[0, flip], recv_p.at[0, flip], (s, mate)).wait_recv()
    keys_of(0)
    pass_on()
    todo = {(0, 0): (1, 2), (1, 0): (3, 4), (1, 1): (5, 6, 7, 8)}
    for seg, chunks in enumerate(SEGMENTS):
        base = chunks[0][0]
        late = len(chunks[-1])
        early = sum(len(c) for c in chunks) - late
        for c, chunk in enumerate(chunks):
            for d in chunk:
                if d > 0:
                    from_mate(d)
            for d in chunk:
                if d > 0:
                    keys_of(d)
            if c < len(chunks) - 1:
                for i in range(groups):
                    score_early(chunk, base, i)
                for d in todo.get((seg, c), ()):
                    forward(d)
                continue
            if seg == len(SEGMENTS) - 1:
                for g in range(groups):
                    wuv_copies[g].wait()

            def half(i, odd, ahead, behind):
                if ahead:
                    score_last(chunk, i + 1, 1 - odd)
                if behind:
                    mix(base, early + late, i - 1, 1 - odd, seg)
                soften(early, late, i, odd, seg)

            def both(j, carry):
                half(2 * j, 0, True, True)
                half(2 * j + 1, 1, True, True)
                return carry

            with jax.named_scope(f"seg{seg}"):
                score_last(chunk, 0, 0)
                half(0, 0, True, False)
                half(1, 1, True, True)
                lax.fori_loop(1, tiles // 4, both, 0)
                for d in todo.get((seg, c), ())[:2]:
                    forward(d)
                lax.fori_loop(tiles // 4, tiles // 2 - 1, both, 0)
                for d in todo.get((seg, c), ())[2:]:
                    forward(d)
                half(tiles - 2, 0, True, True)
                half(tiles - 1, 1, False, True)
                mix(base, early + late, tiles - 1, 1, seg)

    for copy in first:
        copy.wait_send()
    for d in range(1, SLOTS):
        @pl.when(sends_direct(s, d))
        def _():
            for flip in (0, 1):
                outgoing(own, d, flip, s + d).wait_send()

        @pl.when(s >= d)
        def _():
            for flip in (0, 1):
                to_mate(d, flip).wait_send()

        if NEAR < d < SPAN:
            @pl.when(relays(s, d))
            def _():
                for flip in (0, 1):
                    outgoing(own, d, flip, s + d - SPAN).wait_send()


def per_device(n_seq, queries, latent, w_uk, w_uv, doc_lengths):
    heads, nope, rank = w_uk.shape
    vdim = w_uv.shape[2]
    toks = queries.shape[0]
    width = queries.shape[1] // heads
    rope = width - nope
    piece = latent.shape[0]
    groups = 4
    dims = (n_seq, heads, nope, rope, rank, vdim, toks, piece, groups, doc_lengths.shape[0])
    outside = pl.BlockSpec(memory_space=pltpu.HBM)
    dma = pltpu.SemaphoreType.DMA
    all_rows = heads * toks
    tile = TILE * toks
    most = max(sum(len(c) for c in chunks) for chunks in SEGMENTS) * toks
    early = max(sum(len(c) for c in chunks[:-1]) for chunks in SEGMENTS) * toks
    late = max(len(chunks[-1]) for chunks in SEGMENTS) * toks
    return pl.pallas_call(
        functools.partial(kernel, dims),
        out_shape=jax.ShapeDtypeStruct((toks, heads * vdim), jnp.bfloat16),
        in_specs=[pl.BlockSpec(memory_space=pltpu.SMEM)] + [outside] * 4,
        out_specs=pl.BlockSpec(memory_space=pltpu.VMEM),
        scratch_shapes=[
            pltpu.VMEM(queries.shape, jnp.bfloat16),
            pltpu.VMEM(w_uk.shape, jnp.bfloat16),
            pltpu.VMEM(w_uv.shape, jnp.bfloat16),
            pltpu.VMEM((SLOTS, toks, rank + rope), jnp.bfloat16),
            pltpu.VMEM((SLOTS * toks, rank + 256), jnp.bfloat16),
            pltpu.VMEM((all_rows, rank + 256), jnp.bfloat16),
            pltpu.VMEM((all_rows, early), jnp.float32),
            pltpu.VMEM((tile, late), jnp.float32),
            pltpu.VMEM((tile, late), jnp.float32),
            pltpu.VMEM((tile, most), jnp.bfloat16),
            pltpu.VMEM((tile, most), jnp.bfloat16),
            pltpu.VMEM((tile, 128), jnp.float32),
            pltpu.VMEM((tile, 128), jnp.float32),
            pltpu.VMEM((all_rows, 128), jnp.float32),
            pltpu.VMEM((all_rows, 128), jnp.float32),
            pltpu.VMEM((all_rows, rank), jnp.float32),
            pltpu.VMEM((all_rows, 128), jnp.float32),
            dma((groups,)), dma((groups,)), dma((groups,)), dma,
            dma((SLOTS, 2)), dma((SLOTS, 2)), dma((SLOTS, 2)), dma((SLOTS, 2)), dma,
        ],
        compiler_params=pltpu.CompilerParams(
            collective_id=0, has_side_effects=True, vmem_limit_bytes=52 * 1024 * 1024),
    )(doc_lengths, queries, latent, w_uk, w_uv)


def solution(mesh):
    return jax.shard_map(
        functools.partial(per_device, mesh.shape["seq"]),
        mesh=mesh,
        in_specs=(
            P("seq", "heads"),
            P(("seq", "heads"), None),
            P("heads", None, None),
            P("heads", None, None),
            P(),
        ),
        out_specs=P("seq", "heads"),
        check_vma=False,
    )
```

time: 93.3 us -> 38.1 us (0.41)
  the two profiles are of different devices: /device:TPU:128 before, /device:TPU:99 now
where the time goes in v2:
time: 38.1 us; the launch traced here: 37.9 us
  Pallas kernels  35.5 us (93%)
  local copies, waits for them, and re-layouts  2.41 us (6%)
    pallas_call x1, Pallas kernels, per_device(): pl.pallas_call(functools.partial(kernel, dims), out_shape=jax.ShapeDtypeS...  35.5 us
    unnamed x5, local copies, waits for them, and re-layouts  2.41 us

profile of v2, /device:TPU:99, one launch (start us, length us, event | category | flops | bytes accessed | tf_op | source)
XLA Modules:
  0.0 37.9 jit_solution(11253084930423896514)
XLA Ops:
  0.0 0.0 copy-start
  0.0 0.8 %copy-done = bf16[32,576]{1,0:T(8,128)(2,1)S(1)} copy-done((bf16[32,576]{1,0:T(8,128)(2,1)S(1)}, bf16[32,576]{1,0:T(8,128)(2,1)}, u32[]{:S(2)}) %copy-start) | copy-done | bytes 36888
  0.8 0.0 copy-start.1
  0.8 0.7 %copy-done.1 = s32[32]{0:T(128)S(1)} copy-done((s32[32]{0:T(128)S(1)}, s32[32]{0:T(128)}, u32[]{:S(2)}) %copy-start.1) | copy-done | bytes 152
  1.4 35.5 %shard_map.55 = bf16[128,4096]{1,0:T(8,128)(2,1)S(1)} custom-call(s32[32]{0:T(128)S(1)} %copy-done.1, bf16[128,6144]{1,0:T(8,128)(2,1)} %q_hbm.1, bf16[32,576]{1,0:T(8,128)(2,1)S(1)} %copy-done, bf16[32,128,512]{2,1,0:T(8,128)(2,1)} %wuk_hbm.1, bf16[32,512,128]{2,1,0:T(8,128)(2,1)} %wuv_hbm.1), custom_call_target="tpu_custom_call" | custom-call | tf_op jit(solution)/shard_map/pallas_call | solution.py:393
  37.0 1.0 %copy.7 = bf16[128,4096]{1,0:T(8,128)(2,1)} copy(bf16[128,4096]{1,0:T(8,128)(2,1)S(1)} %shard_map.55) | data formatting | bytes 2097152
Async XLA Ops:
  0.0 0.8 %copy-start = (bf16[32,576]{1,0:T(8,128)(2,1)S(1)}, bf16[32,576]{1,0:T(8,128)(2,1)}, u32[]{:S(2)}) copy-start(bf16[32,576]{1,0:T(8,128)(2,1)} %lat_hbm.1) | copy-start | bytes 110596
  0.8 0.7 %copy-start.1 = (s32[32]{0:T(128)S(1)}, s32[32]{0:T(128)}, u32[]{:S(2)}) copy-start(s32[32]{0:T(128)} %doc_ref.1) | copy-start | bytes 388

commit v3 on v2

--- a/solution.py
+++ b/solution.py
@@ -20,7 +20,7 @@
 TILE = 4
 
 
-def kernel(dims, doc_ref, q_hbm, lat_hbm, wuk_hbm, wuv_hbm, out_v,
+def kernel(dims, doc_ref, q_hbm, lat_hbm, wuk_hbm, wuv_hbm, out_v, spare,
            q_v, wuk_v, wuv_v, kv, kk, joined, sc_ref, ring_a, ring_b, p_a, p_b, a_a, a_b, m_ref, l_ref, acc_ref, t_ref,
            q_sem, wuk_sem, wuv_sem, lat_sem,
            send_d, recv_d, send_p, recv_p, send_x):
@@ -266,7 +266,7 @@
                 total = total + l_ref[at, :] * alpha
             if last:
                 inv = 1.0 / jnp.sum(total, axis=1, keepdims=True)
-                a_ref[odd][here, :] = alpha * inv
+                a_ref[odd][here, :] = alpha
                 l_ref[at, :] = jnp.broadcast_to(inv, (STRIP, 128))
             else:
                 l_ref[at, :] = total
@@ -288,16 +288,16 @@
             if seg < len(SEGMENTS) - 1:
                 acc_ref[at, cols] = kept + mixed
                 continue
-            inv = jnp.concatenate([l_ref[at, :]] * (LANES // 128), axis=1)
-            attended.append((kept + mixed * inv).astype(jnp.bfloat16))
+            attended.append((kept + mixed).astype(jnp.bfloat16))
         if seg < len(SEGMENTS) - 1:
             return
         for j in range(TILE):
             h = i * TILE + j
             here = slice(j * toks, (j + 1) * toks)
             whole = jnp.concatenate([x[here] for x in attended], axis=1)
-            out_v[:, pl.ds(pl.multiple_of(h * vdim, vdim), vdim)] = jnp.dot(
-                whole, wuv_v[h], preferred_element_type=jnp.float32).astype(jnp.bfloat16)
+            inv = l_ref[pl.ds(pl.multiple_of(h * toks, toks), toks), :]
+            out_v[:, pl.ds(pl.multiple_of(h * vdim, vdim), vdim)] = (jnp.dot(
+                whole, wuv_v[h], preferred_element_type=jnp.float32) * inv).astype(jnp.bfloat16)
 
     with jax.named_scope("w0"):
         arrived(0, 1)
@@ -392,9 +392,9 @@
     late = max(len(chunks[-1]) for chunks in SEGMENTS) * toks
     return pl.pallas_call(
         functools.partial(kernel, dims),
-        out_shape=jax.ShapeDtypeStruct((toks, heads * vdim), jnp.bfloat16),
+        out_shape=[jax.ShapeDtypeStruct((toks, heads * vdim), jnp.bfloat16)] * 2,
         in_specs=[pl.BlockSpec(memory_space=pltpu.SMEM)] + [outside] * 4,
-        out_specs=pl.BlockSpec(memory_space=pltpu.VMEM),
+        out_specs=[pl.BlockSpec(memory_space=pltpu.VMEM), pl.BlockSpec(memory_space=pl.ANY)],
         scratch_shapes=[
             pltpu.VMEM(queries.shape, jnp.bfloat16),
             pltpu.VMEM(w_uk.shape, jnp.bfloat16),
@@ -417,8 +417,8 @@
             dma((SLOTS, 2)), dma((SLOTS, 2)), dma((SLOTS, 2)), dma((SLOTS, 2)), dma,
         ],
         compiler_params=pltpu.CompilerParams(
-            collective_id=0, has_side_effects=True, vmem_limit_bytes=52 * 1024 * 1024),
-    )(doc_lengths, queries, latent, w_uk, w_uv)
+            collective_id=0, has_side_effects=True, vmem_limit_bytes=(52 * 1024 + 700) * 1024),
+    )(doc_lengths, queries, latent, w_uk, w_uv)[0]
 
 
 def solution(mesh):

time: 38.1 us -> 38 us (level)
  no operation moved by 1% of the time
where the time goes in v3:
time: 38 us; the launch traced here: 37.8 us
  Pallas kernels  35.4 us (93%)
  local copies, waits for them, and re-layouts  2.41 us (6%)
    pallas_call x1, Pallas kernels, per_device(): pl.pallas_call(functools.partial(kernel, dims), out_shape=[jax.ShapeDtype...  35.4 us
    unnamed x5, local copies, waits for them, and re-layouts  2.41 us

profile of v3, /device:TPU:99, one launch (start us, length us, event | category | flops | bytes accessed | tf_op | source)
XLA Modules:
  0.0 37.8 jit_solution(3662398867824901732)
XLA Ops:
  0.0 0.0 copy-start
  0.0 0.8 %copy-done = bf16[32,576]{1,0:T(8,128)(2,1)S(1)} copy-done((bf16[32,576]{1,0:T(8,128)(2,1)S(1)}, bf16[32,576]{1,0:T(8,128)(2,1)}, u32[]{:S(2)}) %copy-start) | copy-done | bytes 36888
  0.8 0.0 copy-start.1
  0.8 0.7 %copy-done.1 = s32[32]{0:T(128)S(1)} copy-done((s32[32]{0:T(128)S(1)}, s32[32]{0:T(128)}, u32[]{:S(2)}) %copy-start.1) | copy-done | bytes 152
  1.4 35.4 %shard_map.55 = (bf16[128,4096]{1,0:T(8,128)(2,1)S(1)}, bf16[128,4096]{1,0:T(8,128)(2,1)}) custom-call(s32[32]{0:T(128)S(1)} %copy-done.1, bf16[128,6144]{1,0:T(8,128)(2,1)} %q_hbm.1, bf16[32,576]{1,0:T(8,128)(2,1)S(1)} %copy-done, bf16[32,128,512]{2,1,0:T(8,128)(2,1)} %wuk_hbm.1, bf16[32,512,128]{2,1,0:T(8,128)(2,1)} %wuv_hbm.1), custom_call_target="tpu_custom_call" | custom-call | tf_op jit(solution)/shard_map/pallas_call | solution.py:393
  36.9 1.0 %copy.7 = bf16[128,4096]{1,0:T(8,128)(2,1)} copy(bf16[128,4096]{1,0:T(8,128)(2,1)S(1)} %get-tuple-element.6) | data formatting | bytes 2097152
Async XLA Ops:
  0.0 0.8 %copy-start = (bf16[32,576]{1,0:T(8,128)(2,1)S(1)}, bf16[32,576]{1,0:T(8,128)(2,1)}, u32[]{:S(2)}) copy-start(bf16[32,576]{1,0:T(8,128)(2,1)} %lat_hbm.1) | copy-start | bytes 110596
  0.8 0.7 %copy-start.1 = (s32[32]{0:T(128)S(1)}, s32[32]{0:T(128)}, u32[]{:S(2)}) copy-start(s32[32]{0:T(128)} %doc_ref.1) | copy-start | bytes 388

commit v4 on v2

--- a/solution.py
+++ b/solution.py
@@ -48,6 +48,41 @@
 
     lat_copy = pltpu.make_async_copy(lat_hbm, kv.at[0, own_rows(hd)], lat_sem)
     lat_copy.start()
+    barrier = pltpu.get_barrier_semaphore()
+
+    def greet(seq, h):
+        pl.semaphore_signal(barrier, inc=1, device_id=(seq, h), device_id_type=MESH)
+
+    def sends_direct(seq, d):
+        inside = seq + d < n_seq
+        if NEAR < d < SPAN:
+            return jnp.logical_and(inside, seq % PLANE + d < PLANE)
+        return inside
+
+    def relays(seq, d):
+        return jnp.logical_and(seq % PLANE + d >= SPAN, seq >= SPAN)
+
+    greet(s, mate)
+    greet(s, holder(1))
+    greet(s, xh_other_mate := (1 - xh) * 2 + (1 - core))
+    for d in range(1, SLOTS):
+        direct_from = s - d
+        ok = jnp.logical_and(s >= d, sends_direct(direct_from, d))
+
+        @pl.when(ok)
+        def _():
+            greet(direct_from, holder(0))
+            greet(direct_from, holder(1))
+
+        if NEAR < d < SPAN:
+            relay_from = s - d + SPAN
+            ok_relay = jnp.logical_and(relay_from < n_seq, relays(relay_from, d))
+
+            @pl.when(ok_relay)
+            def _():
+                greet(relay_from, holder(0))
+                greet(relay_from, holder(1))
+
     q_copies, wuk_copies, wuv_copies = [], [], []
     for g in range(groups):
         cols = pl.ds(g * per * width, per * width)
@@ -57,41 +92,6 @@
         wuv_copies.append(pltpu.make_async_copy(wuv_hbm.at[hs], wuv_v.at[hs], wuv_sem.at[g]))
         q_copies[-1].start()
         wuk_copies[-1].start()
-
-    barrier = pltpu.get_barrier_semaphore()
-
-    def greet(seq, h):
-        pl.semaphore_signal(barrier, inc=1, device_id=(seq, h), device_id_type=MESH)
-
-    def sends_direct(seq, d):
-        inside = seq + d < n_seq
-        if NEAR < d < SPAN:
-            return jnp.logical_and(inside, seq % PLANE + d < PLANE)
-        return inside
-
-    def relays(seq, d):
-        return jnp.logical_and(seq % PLANE + d >= SPAN, seq >= SPAN)
-
-    greet(s, mate)
-    greet(s, holder(1))
-    greet(s, xh_other_mate := (1 - xh) * 2 + (1 - core))
-    for d in range(1, SLOTS):
-        direct_from = s - d
-        ok = jnp.logical_and(s >= d, sends_direct(direct_from, d))
-
-        @pl.when(ok)
-        def _():
-            greet(direct_from, holder(0))
-            greet(direct_from, holder(1))
-
-        if NEAR < d < SPAN:
-            relay_from = s - d + SPAN
-            ok_relay = jnp.logical_and(relay_from < n_seq, relays(relay_from, d))
-
-            @pl.when(ok_relay)
-            def _():
-                greet(relay_from, holder(0))
-                greet(relay_from, holder(1))
 
     expected = jnp.int32(3)
     for d in range(1, SLOTS):
@@ -132,8 +132,7 @@
                 joined[at, rank + 128:rank + 256] = eye
 
     with jax.named_scope("absA"):
-        for g in range(groups // 2):
-            absorb(g)
+        absorb(0)
     with jax.named_scope("bar"):
         lat_copy.wait()
         pl.semaphore_wait(barrier, expected)
@@ -167,16 +166,15 @@
             for flip in flips:
                 outgoing(own, d, flip, s + d).start()
 
-    half = groups // 2
     with jax.named_scope("absB"):
-        absorb(half)
+        absorb(1)
     for d in range(1, NEAR + 1):
         send(d)
     send(SPAN, (0,))
     for g in range(groups):
         wuv_copies[g].start()
     with jax.named_scope("absC"):
-        for g in range(half + 1, groups):
+        for g in range(2, groups):
             absorb(g)
     for d in range(NEAR + 1, SPAN):
         send(d)

time: 38.1 us -> 38.8 us (1.018)
  Pallas kernels: 35.5 us -> 36.2 us
    pallas_call x1, Pallas kernels: 35.5 us -> 36.2 us  [per_device(): pl.pallas_call(functools.partial(kernel, dims), out_shape=jax.ShapeDtypeS...]
where the time goes in v4:
time: 38.8 us; the launch traced here: 38.6 us
  Pallas kernels  36.2 us (93%)
  local copies, waits for them, and re-layouts  2.41 us (6%)
    pallas_call x1, Pallas kernels, per_device(): pl.pallas_call(functools.partial(kernel, dims), out_shape=jax.ShapeDtypeS...  36.2 us
    unnamed x5, local copies, waits for them, and re-layouts  2.41 us

profile of v4, /device:TPU:99, one launch (start us, length us, event | category | flops | bytes accessed | tf_op | source)
XLA Modules:
  0.0 38.6 jit_solution(3183713346426594589)
XLA Ops:
  0.0 0.0 copy-start
  0.0 0.8 %copy-done = bf16[32,576]{1,0:T(8,128)(2,1)S(1)} copy-done((bf16[32,576]{1,0:T(8,128)(2,1)S(1)}, bf16[32,576]{1,0:T(8,128)(2,1)}, u32[]{:S(2)}) %copy-start) | copy-done | bytes 36888
  0.8 0.0 copy-start.1
  0.8 0.7 %copy-done.1 = s32[32]{0:T(128)S(1)} copy-done((s32[32]{0:T(128)S(1)}, s32[32]{0:T(128)}, u32[]{:S(2)}) %copy-start.1) | copy-done | bytes 152
  1.4 36.2 %shard_map.55 = bf16[128,4096]{1,0:T(8,128)(2,1)S(1)} custom-call(s32[32]{0:T(128)S(1)} %copy-done.1, bf16[128,6144]{1,0:T(8,128)(2,1)} %q_hbm.1, bf16[32,576]{1,0:T(8,128)(2,1)S(1)} %copy-done, bf16[32,128,512]{2,1,0:T(8,128)(2,1)} %wuk_hbm.1, bf16[32,512,128]{2,1,0:T(8,128)(2,1)} %wuv_hbm.1), custom_call_target="tpu_custom_call" | custom-call | tf_op jit(solution)/shard_map/pallas_call | solution.py:391
  37.7 1.0 %copy.7 = bf16[128,4096]{1,0:T(8,128)(2,1)} copy(bf16[128,4096]{1,0:T(8,128)(2,1)S(1)} %shard_map.55) | data formatting | bytes 2097152
Async XLA Ops:
  0.0 0.8 %copy-start = (bf16[32,576]{1,0:T(8,128)(2,1)S(1)}, bf16[32,576]{1,0:T(8,128)(2,1)}, u32[]{:S(2)}) copy-start(bf16[32,576]{1,0:T(8,128)(2,1)} %lat_hbm.1) | copy-start | bytes 110596
  0.8 0.7 %copy-start.1 = (s32[32]{0:T(128)S(1)}, s32[32]{0:T(128)}, u32[]{:S(2)}) copy-start(s32[32]{0:T(128)} %doc_ref.1) | copy-start | bytes 388
